TPU v7x, 32 devices: a whole 2x2x4 slice. The times are simulated.
32 devices in a mesh: row: 8 (over z, core), col: 4 (over y, x).
Axes of the slice: x: 2, y: 2, z: 4, core: 2. Of those that a mesh axis runs over, the one named last changes fastest.
Arguments:
- wrapped_phase: float32 [16384, 2048], P('row', 'col'), may hold values from -2.85 to 2.85, as said below
Outputs:
- unwrapped: float32 [16384, 2048], P('row', 'col')
Inputs may be any that keep to these rules, and one draw needn't show every extreme that they name: The difference of wrapped_phase between any two adjacent cells of the map lies 0.14 or more away from every odd multiple of pi.
All inputs are finite; a program needn't handle non-finite values.
Results may differ from a plain program's by a relative error of at most 0.0003.
Values sent between devices are 32-bit elements; how exact they have to be, the bound alone decides.
A program may use at most 128 MiB of HBM per device.

v0:
```python
import functools
import math

import jax
import jax.numpy as jnp
import numpy as np
from jax import lax
from jax.experimental import pallas as pl
from jax.experimental.pallas import tpu as pltpu
from jax.sharding import PartitionSpec as P

TILE = 256
FULL_TURN = 2.0 * math.pi
MESH = pl.DeviceIdType.MESH
LANES = 128


def wrap_angle(values):
    return values - FULL_TURN * jnp.floor(values * (1.0 / FULL_TURN) + 0.5)


def cos32(angle):
    return np.cos(angle.astype(np.float64)).astype(np.float32)


def tables(length):
    f32 = np.float32
    order = np.arange(length, dtype=f32)
    angle = (f32(math.pi) * order)[:, None] * (f32(2) * order + f32(1))[None, :] / f32(2 * length)
    cosine = cos32(angle) * f32(math.sqrt(2.0 / length))
    cosine[0] = cosine[0] * f32(math.sqrt(0.5))
    wave = f32(2) * cos32(f32(math.pi) * order / f32(length))
    eigen = (wave[:, None] + wave[None, :]) - f32(4)
    eigen[0, 0] = -1
    inverse = 1.0 / eigen.astype(np.float64)
    inverse[0, 0] = 0
    c64 = cosine.astype(np.float64)
    weights = []
    for cell in (length - 1, 0):
        green = (c64[:, cell] * inverse[0]) @ c64
        step = green - np.append(green[1:], 0.0)
        step[-1] = 0
        weights.append(step / length)
    return cosine, inverse.astype(f32), np.stack(weights).astype(f32)


def split(values):
    high = values.astype(jnp.bfloat16)
    low = (values - high.astype(jnp.float32)).astype(jnp.bfloat16)
    return high, low


def dot(left, right):
    return jnp.dot(left, right, preferred_element_type=jnp.float32)


def times_right(values, table):
    high, low = split(values)
    return dot(jnp.concatenate([high, low, high], 1), table)


def times_left(table, values):
    high, low = split(values)
    return dot(table, jnp.concatenate([high, low, high], 0))


def slopes(band):
    rows, width = band.shape
    down = wrap_angle(pltpu.roll(band, rows - 1, 0) - band)
    across = wrap_angle(pltpu.roll(band, width - 1, 1) - band)
    return down, across


def solve_kernel(x_ref, off_ref, left1, right1, left2, right2, inv_ref, out_ref):
    index = pl.program_id(0)
    band = x_ref[...]
    rows, width = band.shape
    down, across = slopes(band)
    row_id = lax.broadcasted_iota(jnp.int32, band.shape, 0)
    col_id = lax.broadcasted_iota(jnp.int32, band.shape, 1) % TILE
    down = jnp.where(row_id == TILE - 1, 0.0, down)
    across = jnp.where(col_id == TILE - 1, 0.0, across)
    diverge = down - pltpu.roll(down, 1, 0) + across - pltpu.roll(across, 1, 1)
    for t in range(width // TILE):
        cols = slice(t * TILE, (t + 1) * TILE)
        inner = times_right(diverge[:, cols], right1[...])
        scaled = times_left(left1[...], inner) * inv_ref[...]
        inner = times_right(scaled, right2[...])
        solved = times_left(left2[...], inner)
        out_ref[:, cols] = solved + off_ref[pl.ds(index, 1), cols]


def lane_sum(values):
    return jnp.sum(values, axis=1, keepdims=True)


def running(values):
    n = values.shape[0]
    row = lax.broadcasted_iota(jnp.int32, values.shape, 0)
    total = jnp.zeros_like(values)
    for k in range(n - 1):
        total = total + jnp.where(row > k, values[k : k + 1], 0.0)
    return total


def chain_kernel(
    n_row, n_col, x_ref, w_ref, off_ref,
    col_out, col_in, top_out, top_in, sum_s, sum_d, first_s, last_s,
    down_out, down_in, row_out, row_in,
    edge_send, edge_recv, down_send, down_recv, row_send, row_recv,
):
    r, c = lax.axis_index("row"), lax.axis_index("col")
    height, width = x_ref.shape
    bands, tiles = height // TILE, width // TILE

    barrier = pltpu.get_barrier_semaphore()
    for k in range(1, n_row):
        pl.semaphore_signal(barrier, inc=1, device_id=(lax.rem(r + k, n_row), c), device_id_type=MESH)
    for k in range(1, n_col):
        pl.semaphore_signal(barrier, inc=1, device_id=(r, lax.rem(c + k, n_col)), device_id_type=MESH)

    for i in range(bands):
        rows = pl.ds(i * TILE, TILE)
        col_out[i : i + 1, :] = jnp.transpose(x_ref[rows, 0:LANES])[0:1, :]
    top_out[...] = jnp.broadcast_to(x_ref[0:1, 0:TILE], top_out.shape)

    pl.semaphore_wait(barrier, n_row + n_col - 2)
    edge_col = pltpu.make_async_remote_copy(
        src_ref=col_out, dst_ref=col_in, send_sem=edge_send.at[0], recv_sem=edge_recv.at[0],
        device_id=(r, lax.rem(c + n_col - 1, n_col)), device_id_type=MESH)
    edge_top = pltpu.make_async_remote_copy(
        src_ref=top_out, dst_ref=top_in, send_sem=edge_send.at[1], recv_sem=edge_recv.at[1],
        device_id=(lax.rem(r + n_row - 1, n_row), c), device_id_type=MESH)
    edge_col.start()
    edge_top.start()

    for i in range(bands):
        rows = pl.ds(i * TILE, TILE)
        band = x_ref[rows, :]
        across = wrap_angle(pltpu.roll(band, width - 1, 1) - band)
        sum_s[i : i + 1, :] = jnp.sum(across, axis=0, keepdims=True)
        first = band[:, 0:TILE]
        down = wrap_angle(pltpu.roll(first, TILE - 1, 0) - first)
        weight = w_ref[:, 2 * TILE : 2 * TILE + 2]
        sum_d[i : i + 1, :] = jnp.sum(down * weight[:, 0:1], axis=0, keepdims=True)
        sum_d[bands + i : bands + i + 1, :] = jnp.sum(down * weight[:, 1:2], axis=0, keepdims=True)
        first_s[i : i + 1, :] = first[0:1, :]
        last_s[i : i + 1, :] = first[TILE - 1 : TILE, :]
        last_col = jnp.transpose(x_ref[rows, width - LANES : width])
        last_s[bands + i : bands + i + 1, :] = last_col[LANES - 1 : LANES, :]

    scale = 1.0 / TILE
    down_last = lane_sum(sum_d[0:bands, :])
    down_first = lane_sum(sum_d[bands : 2 * bands, :])
    edge_top.wait()
    edge_col.wait()
    below = jnp.concatenate([first_s[1:bands, :], top_in[0:1, :]], 0)
    border = lane_sum(wrap_angle(below - last_s[0:bands, :])) * scale
    band_id = lax.broadcasted_iota(jnp.int32, (bands, 1), 0)
    next_first = jnp.concatenate([down_first[1:bands], down_first[0:1]], 0)
    jump = down_last + border - next_first
    jump_total = jnp.sum(jump, axis=0, keepdims=True)
    starts = running(jump)
    lane = lax.broadcasted_iota(jnp.int32, (8, LANES), 1)
    down_first0 = down_first[0:1]
    down_out[...] = jnp.where(lane == 0, jump_total, jnp.where(lane == 1, down_first0, 0.0))
    copies = []
    for k in range(1, n_row):
        copies.append(pltpu.make_async_remote_copy(
            src_ref=down_out, dst_ref=down_in.at[k - 1],
            send_sem=down_send.at[k - 1], recv_sem=down_recv.at[k - 1],
            device_id=(lax.rem(r + k, n_row), c), device_id_type=MESH))
    for copy in copies:
        copy.start()

    sums = sum_s[...]
    last_w, first_w = w_ref[0:1, 0:TILE], w_ref[0:1, TILE : 2 * TILE]
    lasts = [lane_sum(sums[:, t * TILE : (t + 1) * TILE] * last_w) for t in range(tiles)]
    firsts = [lane_sum(sums[:, t * TILE : (t + 1) * TILE] * first_w) for t in range(tiles)]
    along = [jnp.zeros((bands, 1), jnp.float32)]
    for t in range(tiles - 1):
        end = (t + 1) * TILE
        along.append(along[-1] + lasts[t] + sums[:, end - 1 : end] * scale - firsts[t + 1])
    edge = lane_sum(wrap_angle(col_in[...] - last_s[bands : 2 * bands, :])) * scale
    row_total = along[-1] + lasts[-1] + edge - firsts[0]

    for copy in copies:
        copy.wait()
    above = jnp.zeros((1, 1), jnp.float32)
    origin = jnp.where(r == 0, down_first0, 0.0)
    for k in range(1, n_row):
        got = down_in[k - 1]
        above = above + jnp.where(k <= r, got[0:1, 0:1], 0.0)
        origin = origin + jnp.where(k == r, got[0:1, 1:2], 0.0)
    starts = starts + above + origin - down_first0

    lane = lax.broadcasted_iota(jnp.int32, (bands, LANES), 1)
    row_out[...] = jnp.where(
        lane == 0, row_total, jnp.where(lane == 1, starts + firsts[0], 0.0))
    copies = []
    for k in range(1, n_col):
        copies.append(pltpu.make_async_remote_copy(
            src_ref=row_out, dst_ref=row_in.at[k - 1],
            send_sem=row_send.at[k - 1], recv_sem=row_recv.at[k - 1],
            device_id=(r, lax.rem(c + k, n_col)), device_id_type=MESH))
    for copy in copies:
        copy.start()
    for copy in copies:
        copy.wait()
    offset = jnp.where(c == 0, starts + firsts[0], 0.0) - firsts[0]
    for k in range(1, n_col):
        got = row_in[k - 1]
        offset = offset + jnp.where(k <= c, got[:, 0:1], 0.0)
        offset = offset + jnp.where(k == c, got[:, 1:2], 0.0)
    for t in range(tiles):
        off_ref[:, t * TILE : (t + 1) * TILE] = jnp.broadcast_to(offset + along[t], (bands, TILE))


def per_device(n_row, n_col, x):
    height, width = x.shape
    bands = height // TILE
    cosine, inverse, weights = tables(TILE)
    high = cosine.astype(jnp.bfloat16)
    low = (cosine - high.astype(np.float32)).astype(jnp.bfloat16)
    across = lambda h, l: np.concatenate([h, h, l], 1)
    along = lambda h, l: np.concatenate([h, h, l], 0)
    left1, right1 = across(high, low), along(high.T, low.T)
    left2, right2 = across(high.T, low.T), along(high, low)
    w = np.zeros((TILE, 2 * TILE + LANES), np.float32)
    w[:, 0:TILE] = weights[0]
    w[:, TILE : 2 * TILE] = weights[1]
    w[:, 2 * TILE] = weights[0]
    w[:, 2 * TILE + 1] = weights[1]

    vmem = pl.BlockSpec(memory_space=pltpu.VMEM)
    f32 = jnp.float32
    offsets = pl.pallas_call(
        functools.partial(chain_kernel, n_row, n_col),
        out_shape=jax.ShapeDtypeStruct((bands, width), f32),
        in_specs=[vmem, vmem],
        out_specs=vmem,
        scratch_shapes=[
            pltpu.VMEM((bands, TILE), f32),
            pltpu.VMEM((bands, TILE), f32),
            pltpu.VMEM((8, TILE), f32),
            pltpu.VMEM((8, TILE), f32),
            pltpu.VMEM((bands, width), f32),
            pltpu.VMEM((2 * bands, TILE), f32),
            pltpu.VMEM((bands, TILE), f32),
            pltpu.VMEM((2 * bands, TILE), f32),
            pltpu.VMEM((8, LANES), f32),
            pltpu.VMEM((n_row - 1, 8, LANES), f32),
            pltpu.VMEM((bands, LANES), f32),
            pltpu.VMEM((n_col - 1, bands, LANES), f32),
            pltpu.SemaphoreType.DMA((2,)),
            pltpu.SemaphoreType.DMA((2,)),
            pltpu.SemaphoreType.DMA((n_row - 1,)),
            pltpu.SemaphoreType.DMA((n_row - 1,)),
            pltpu.SemaphoreType.DMA((n_col - 1,)),
            pltpu.SemaphoreType.DMA((n_col - 1,)),
        ],
        compiler_params=pltpu.CompilerParams(collective_id=0, has_side_effects=True),
        name="chain",
    )(x, jnp.asarray(w))

    whole = lambda a: pl.BlockSpec(a.shape, lambda i: (0,) * len(a.shape))
    consts = [jnp.asarray(a) for a in (left1, right1, left2, right2, inverse)]
    return pl.pallas_call(
        solve_kernel,
        grid=(bands,),
        out_shape=jax.ShapeDtypeStruct(x.shape, f32),
        in_specs=[pl.BlockSpec((TILE, width), lambda i: (i, 0)), whole(offsets)]
        + [whole(a) for a in consts],
        out_specs=pl.BlockSpec((TILE, width), lambda i: (i, 0)),
        compiler_params=pltpu.CompilerParams(dimension_semantics=("arbitrary",)),
        name="solve",
    )(x, offsets, *consts)


def solution(mesh):
    n_row, n_col = mesh.shape["row"], mesh.shape["col"]
    return jax.shard_map(
        functools.partial(per_device, n_row, n_col), mesh=mesh,
        in_specs=(P("row", "col"),), out_specs=P("row", "col"), check_vma=False,
    )
```

profile of v0, /device:TPU:0, one launch (start us, length us, event | category | flops | bytes accessed | tf_op | source)
XLA Modules:
  0.0 40.1 jit_solution(11444468192296483353)
XLA Ops:
  0.0 19.0 %chain.1.off_ref = f32[8,512]{1,0:T(8,128)} custom-call(f32[2048,512]{1,0:T(8,128)} %x_ref.3, f32[256,640]{1,0:T(8,128)} %constant.12.clone.w_ref), custom_call_target="tpu_custom_call" | custom-call | tf_op jit(solution)/shard_map/chain/pallas_call | solution.py:237
  19.0 21.2 %solve.1 = f32[2048,512]{1,0:T(8,128)} custom-call(f32[2048,512]{1,0:T(8,128)} %x_ref.3, f32[8,512]{1,0:T(8,128)} %chain.1.off_ref, bf16[256,768]{1,0:T(8,128)(2,1)} %constant.13.clone.left1, bf16[768,256]{1,0:T(8,128)(2,1)} %constant.14.clone.right1, bf16[256,768]{1,0:T(8,128)(2,1)} %constant.15.clone.left2, bf16[768,256]{1,0:T(8,128)(2,1)} %constant.16.clone.right2, ...), custom_call_target="tpu_custom_call" | custom-call | tf_op jit(solution)/shard_map/solve/pallas_call | solution.py:268
where the time goes:
time: 40.3 us; the launch traced here: 40.1 us
  Pallas kernels  40.1 us (100%)
    pallas_call x1, Pallas kernels, per_device(): pl.pallas_call(solve_kernel, grid=(bands,), out_shape=jax.ShapeDtypeStruc...  21.2 us
    pallas_call x1, Pallas kernels, per_device(): pl.pallas_call(functools.partial(chain_kernel, n_row, n_col), out_shape=j...  19 us

commit v1 on v0

--- a/solution.py
+++ b/solution.py
@@ -54,40 +54,51 @@
     return jnp.dot(left, right, preferred_element_type=jnp.float32)
 
 
-def times_right(values, table):
-    high, low = split(values)
-    return dot(jnp.concatenate([high, low, high], 1), table)
-
-
-def times_left(table, values):
-    high, low = split(values)
-    return dot(table, jnp.concatenate([high, low, high], 0))
-
-
-def slopes(band):
-    rows, width = band.shape
-    down = wrap_angle(pltpu.roll(band, rows - 1, 0) - band)
-    across = wrap_angle(pltpu.roll(band, width - 1, 1) - band)
-    return down, across
-
-
-def solve_kernel(x_ref, off_ref, left1, right1, left2, right2, inv_ref, out_ref):
-    index = pl.program_id(0)
-    band = x_ref[...]
-    rows, width = band.shape
-    down, across = slopes(band)
-    row_id = lax.broadcasted_iota(jnp.int32, band.shape, 0)
-    col_id = lax.broadcasted_iota(jnp.int32, band.shape, 1) % TILE
-    down = jnp.where(row_id == TILE - 1, 0.0, down)
-    across = jnp.where(col_id == TILE - 1, 0.0, across)
-    diverge = down - pltpu.roll(down, 1, 0) + across - pltpu.roll(across, 1, 1)
-    for t in range(width // TILE):
-        cols = slice(t * TILE, (t + 1) * TILE)
-        inner = times_right(diverge[:, cols], right1[...])
-        scaled = times_left(left1[...], inner) * inv_ref[...]
-        inner = times_right(scaled, right2[...])
-        solved = times_left(left2[...], inner)
-        out_ref[:, cols] = solved + off_ref[pl.ds(index, 1), cols]
+def stack3(high, low, axis):
+    return jnp.concatenate([high, low, high], axis)
+
+
+def sandwich(high, low, right, left):
+    n = high.shape[0]
+    table = right[...]
+    inner = dot(stack3(high, low, 1), jnp.concatenate([table[:n], table], 0))
+    high, low = split(inner)
+    table = left[...]
+    return dot(jnp.concatenate([table[:, :n], table], 1), stack3(high, low, 0))
+
+
+def band_rows(i):
+    return pl.ds(pl.multiple_of(i * TILE, TILE), TILE)
+
+
+def band_copy(src, dst, sem, i):
+    rows = band_rows(i)
+    return pltpu.make_async_copy(src.at[rows, :], dst.at[rows, :], sem.at[i])
+
+
+def finish_kernel(
+    high_hbm, low_hbm, off_ref, left, right, out_hbm, high_s, low_s, out_s, high_sem, low_sem, out_sem
+):
+    height, width = out_s.shape
+    bands, tiles = height // TILE, width // TILE
+    for i in range(bands):
+        band_copy(high_hbm, high_s, high_sem, i).start()
+        band_copy(low_hbm, low_s, low_sem, i).start()
+
+    def step(i, carry):
+        rows = band_rows(i)
+        band_copy(high_hbm, high_s, high_sem, i).wait()
+        band_copy(low_hbm, low_s, low_sem, i).wait()
+        for t in range(tiles):
+            cols = slice(t * TILE, (t + 1) * TILE)
+            solved = sandwich(high_s[rows, cols], low_s[rows, cols], right, left)
+            out_s[rows, cols] = solved + off_ref[pl.ds(i, 1), cols]
+        band_copy(out_s, out_hbm, out_sem, i).start()
+        return carry
+
+    lax.fori_loop(0, bands, step, 0)
+    for i in range(bands):
+        band_copy(out_s, out_hbm, out_sem, i).wait()
 
 
 def lane_sum(values):
@@ -103,15 +114,60 @@
     return total
 
 
+CHUNK = 32
+
+
+def slope_band(x_s, w_ref, i, bands, dh_s, dl_s, sum_s, sum_d, first_s, last_s):
+    width = x_s.shape[1]
+    base = pl.multiple_of(i * TILE, TILE)
+    shape = (CHUNK, width)
+    row_id = lax.broadcasted_iota(jnp.int32, shape, 0)
+    tile_end = lax.broadcasted_iota(jnp.int32, shape, 1) % TILE == TILE - 1
+    fold = lambda v: jnp.sum(v.reshape(CHUNK // 8, 8, v.shape[1]), axis=0)
+    acc = jnp.zeros((8, width), jnp.float32)
+    acc_last = jnp.zeros((8, TILE), jnp.float32)
+    acc_first = jnp.zeros((8, TILE), jnp.float32)
+    before = jnp.zeros((1, width), jnp.float32)
+    for k in range(TILE // CHUNK):
+        rows = pl.ds(base + k * CHUNK, CHUNK)
+        x = x_s[rows, :]
+        below = pltpu.roll(x, CHUNK - 1, 0)
+        if k < TILE // CHUNK - 1:
+            below = jnp.where(row_id == CHUNK - 1, x_s[pl.ds(base + (k + 1) * CHUNK, 1), :], below)
+        down = wrap_angle(below - x)
+        if k == TILE // CHUNK - 1:
+            down = jnp.where(row_id == CHUNK - 1, 0.0, down)
+        across = wrap_angle(pltpu.roll(x, width - 1, 1) - x)
+        acc = acc + fold(across)
+        weight = w_ref[k * CHUNK : (k + 1) * CHUNK, 2 * TILE : 2 * TILE + 2]
+        acc_last = acc_last + fold(down[:, :TILE] * weight[:, 0:1])
+        acc_first = acc_first + fold(down[:, :TILE] * weight[:, 1:2])
+        across = jnp.where(tile_end, 0.0, across)
+        above = jnp.where(row_id == 0, before, pltpu.roll(down, 1, 0))
+        before = down[CHUNK - 1 : CHUNK, :]
+        high, low = split(down - above + across - pltpu.roll(across, 1, 1))
+        dh_s[rows, :] = high
+        dl_s[rows, :] = low
+    sum_s[pl.ds(i, 1), :] = jnp.sum(acc, axis=0, keepdims=True)
+    sum_d[pl.ds(i, 1), :] = jnp.sum(acc_last, axis=0, keepdims=True)
+    sum_d[pl.ds(bands + i, 1), :] = jnp.sum(acc_first, axis=0, keepdims=True)
+    first_s[pl.ds(i, 1), :] = x_s[pl.ds(base, 1), 0:TILE]
+    last_s[pl.ds(i, 1), :] = x_s[pl.ds(base + TILE - 1, 1), 0:TILE]
+
+
 def chain_kernel(
-    n_row, n_col, x_ref, w_ref, off_ref,
+    n_row, n_col, x_hbm, w_ref, left, right, inv_ref, high_hbm, low_hbm, off_ref,
+    x_s, dh_s, dl_s, sh_s, sl_s,
     col_out, col_in, top_out, top_in, sum_s, sum_d, first_s, last_s,
     down_out, down_in, row_out, row_in,
     edge_send, edge_recv, down_send, down_recv, row_send, row_recv,
+    x_sem, high_sem, low_sem,
 ):
     r, c = lax.axis_index("row"), lax.axis_index("col")
-    height, width = x_ref.shape
+    height, width = x_s.shape
     bands, tiles = height // TILE, width // TILE
+    for i in range(bands):
+        band_copy(x_hbm, x_s, x_sem, i).start()
 
     barrier = pltpu.get_barrier_semaphore()
     for k in range(1, n_row):
@@ -119,10 +175,16 @@
     for k in range(1, n_col):
         pl.semaphore_signal(barrier, inc=1, device_id=(r, lax.rem(c + k, n_col)), device_id_type=MESH)
 
-    for i in range(bands):
-        rows = pl.ds(i * TILE, TILE)
-        col_out[i : i + 1, :] = jnp.transpose(x_ref[rows, 0:LANES])[0:1, :]
-    top_out[...] = jnp.broadcast_to(x_ref[0:1, 0:TILE], top_out.shape)
+    def take_columns(i, carry):
+        band_copy(x_hbm, x_s, x_sem, i).wait()
+        rows = band_rows(i)
+        col_out[pl.ds(i, 1), :] = jnp.transpose(x_s[rows, 0:LANES])[0:1, :]
+        ends = jnp.transpose(x_s[rows, width - LANES : width])
+        last_s[pl.ds(bands + i, 1), :] = ends[LANES - 1 : LANES, :]
+        return carry
+
+    lax.fori_loop(0, bands, take_columns, 0)
+    top_out[...] = jnp.broadcast_to(x_s[0:1, 0:TILE], top_out.shape)
 
     pl.semaphore_wait(barrier, n_row + n_col - 2)
     edge_col = pltpu.make_async_remote_copy(
@@ -134,20 +196,21 @@
     edge_col.start()
     edge_top.start()
 
-    for i in range(bands):
-        rows = pl.ds(i * TILE, TILE)
-        band = x_ref[rows, :]
-        across = wrap_angle(pltpu.roll(band, width - 1, 1) - band)
-        sum_s[i : i + 1, :] = jnp.sum(across, axis=0, keepdims=True)
-        first = band[:, 0:TILE]
-        down = wrap_angle(pltpu.roll(first, TILE - 1, 0) - first)
-        weight = w_ref[:, 2 * TILE : 2 * TILE + 2]
-        sum_d[i : i + 1, :] = jnp.sum(down * weight[:, 0:1], axis=0, keepdims=True)
-        sum_d[bands + i : bands + i + 1, :] = jnp.sum(down * weight[:, 1:2], axis=0, keepdims=True)
-        first_s[i : i + 1, :] = first[0:1, :]
-        last_s[i : i + 1, :] = first[TILE - 1 : TILE, :]
-        last_col = jnp.transpose(x_ref[rows, width - LANES : width])
-        last_s[bands + i : bands + i + 1, :] = last_col[LANES - 1 : LANES, :]
+    def slope_step(i, carry):
+        slope_band(x_s, w_ref, i, bands, dh_s, dl_s, sum_s, sum_d, first_s, last_s)
+        return carry
+
+    lax.fori_loop(0, bands, slope_step, 0)
+
+    def spectrum_step(i, carry):
+        rows = band_rows(i)
+        for t in range(tiles):
+            cols = slice(t * TILE, (t + 1) * TILE)
+            scaled = sandwich(dh_s[rows, cols], dl_s[rows, cols], right, left) * inv_ref[...]
+            sh_s[rows, cols], sl_s[rows, cols] = split(scaled)
+        band_copy(sh_s, high_hbm, high_sem, i).start()
+        band_copy(sl_s, low_hbm, low_sem, i).start()
+        return carry
 
     scale = 1.0 / TILE
     down_last = lane_sum(sum_d[0:bands, :])
@@ -184,6 +247,7 @@
     edge = lane_sum(wrap_angle(col_in[...] - last_s[bands : 2 * bands, :])) * scale
     row_total = along[-1] + lasts[-1] + edge - firsts[0]
 
+    lax.fori_loop(0, bands // 2, spectrum_step, 0)
     for copy in copies:
         copy.wait()
     above = jnp.zeros((1, 1), jnp.float32)
@@ -205,6 +269,7 @@
             device_id=(r, lax.rem(c + k, n_col)), device_id_type=MESH))
     for copy in copies:
         copy.start()
+    lax.fori_loop(bands // 2, bands, spectrum_step, 0)
     for copy in copies:
         copy.wait()
     offset = jnp.where(c == 0, starts + firsts[0], 0.0) - firsts[0]
@@ -214,6 +279,9 @@
         offset = offset + jnp.where(k == c, got[:, 1:2], 0.0)
     for t in range(tiles):
         off_ref[:, t * TILE : (t + 1) * TILE] = jnp.broadcast_to(offset + along[t], (bands, TILE))
+    for i in range(bands):
+        band_copy(sh_s, high_hbm, high_sem, i).wait()
+        band_copy(sl_s, low_hbm, low_sem, i).wait()
 
 
 def per_device(n_row, n_col, x):
@@ -222,10 +290,9 @@
     cosine, inverse, weights = tables(TILE)
     high = cosine.astype(jnp.bfloat16)
     low = (cosine - high.astype(np.float32)).astype(jnp.bfloat16)
-    across = lambda h, l: np.concatenate([h, h, l], 1)
-    along = lambda h, l: np.concatenate([h, h, l], 0)
-    left1, right1 = across(high, low), along(high.T, low.T)
-    left2, right2 = across(high.T, low.T), along(high, low)
+    beside, over = np.concatenate([high, low], 1), np.concatenate([high, low], 0)
+    beside_t = np.concatenate([high.T, low.T], 1)
+    over_t = np.concatenate([high.T, low.T], 0)
     w = np.zeros((TILE, 2 * TILE + LANES), np.float32)
     w[:, 0:TILE] = weights[0]
     w[:, TILE : 2 * TILE] = weights[1]
@@ -233,13 +300,23 @@
     w[:, 2 * TILE + 1] = weights[1]
 
     vmem = pl.BlockSpec(memory_space=pltpu.VMEM)
-    f32 = jnp.float32
-    offsets = pl.pallas_call(
+    anywhere = pl.BlockSpec(memory_space=pl.ANY)
+    f32, bf16 = jnp.float32, jnp.bfloat16
+    high_s, low_s, offsets = pl.pallas_call(
         functools.partial(chain_kernel, n_row, n_col),
-        out_shape=jax.ShapeDtypeStruct((bands, width), f32),
-        in_specs=[vmem, vmem],
-        out_specs=vmem,
+        out_shape=[
+            jax.ShapeDtypeStruct(x.shape, bf16),
+            jax.ShapeDtypeStruct(x.shape, bf16),
+            jax.ShapeDtypeStruct((bands, width), f32),
+        ],
+        in_specs=[anywhere] + [vmem] * 4,
+        out_specs=[anywhere, anywhere, vmem],
         scratch_shapes=[
+            pltpu.VMEM((height, width), f32),
+            pltpu.VMEM((height, width), bf16),
+            pltpu.VMEM((height, width), bf16),
+            pltpu.VMEM((height, width), bf16),
+            pltpu.VMEM((height, width), bf16),
             pltpu.VMEM((bands, TILE), f32),
             pltpu.VMEM((bands, TILE), f32),
             pltpu.VMEM((8, TILE), f32),
@@ -258,23 +335,29 @@
             pltpu.SemaphoreType.DMA((n_row - 1,)),
             pltpu.SemaphoreType.DMA((n_col - 1,)),
             pltpu.SemaphoreType.DMA((n_col - 1,)),
+            pltpu.SemaphoreType.DMA((bands,)),
+            pltpu.SemaphoreType.DMA((bands,)),
+            pltpu.SemaphoreType.DMA((bands,)),
         ],
         compiler_params=pltpu.CompilerParams(collective_id=0, has_side_effects=True),
         name="chain",
-    )(x, jnp.asarray(w))
-
-    whole = lambda a: pl.BlockSpec(a.shape, lambda i: (0,) * len(a.shape))
-    consts = [jnp.asarray(a) for a in (left1, right1, left2, right2, inverse)]
+    )(x, jnp.asarray(w), jnp.asarray(beside), jnp.asarray(over_t), jnp.asarray(inverse))
+
     return pl.pallas_call(
-        solve_kernel,
-        grid=(bands,),
+        finish_kernel,
         out_shape=jax.ShapeDtypeStruct(x.shape, f32),
-        in_specs=[pl.BlockSpec((TILE, width), lambda i: (i, 0)), whole(offsets)]
-        + [whole(a) for a in consts],
-        out_specs=pl.BlockSpec((TILE, width), lambda i: (i, 0)),
-        compiler_params=pltpu.CompilerParams(dimension_semantics=("arbitrary",)),
-        name="solve",
-    )(x, offsets, *consts)
+        in_specs=[anywhere, anywhere, vmem, vmem, vmem],
+        out_specs=anywhere,
+        scratch_shapes=[
+            pltpu.VMEM((height, width), bf16),
+            pltpu.VMEM((height, width), bf16),
+            pltpu.VMEM((height, width), f32),
+            pltpu.SemaphoreType.DMA((bands,)),
+            pltpu.SemaphoreType.DMA((bands,)),
+            pltpu.SemaphoreType.DMA((bands,)),
+        ],
+        name="finish",
+    )(high_s, low_s, offsets, jnp.asarray(beside_t), jnp.asarray(over))
 
 
 def solution(mesh):

time: 40.3 us -> 32.3 us (0.80)
  Pallas kernels: 40.1 us -> 32.1 us
    pallas_call x2, Pallas kernels: 40.1 us -> 32.1 us  [the longest x1 22 us: per_device(): pl.pallas_call(functools.partial(chain_kernel, n_row, n_col), out_shape=[...]
where the time goes in v1:
time: 32.3 us; the launch traced here: 32.1 us
  Pallas kernels  32.1 us (99%)
    pallas_call x1, Pallas kernels, per_device(): pl.pallas_call(functools.partial(chain_kernel, n_row, n_col), out_shape=[...  22 us
    pallas_call x1, Pallas kernels, per_device(): pl.pallas_call(finish_kernel, out_shape=jax.ShapeDtypeStruct(x.shape, f32...  10.1 us

profile of v1, /device:TPU:0, one launch (start us, length us, event | category | flops | bytes accessed | tf_op | source)
XLA Modules:
  0.0 32.1 jit_solution(3897290055843243752)
XLA Ops:
  0.0 22.0 %chain.1 = (bf16[2048,512]{1,0:T(8,128)(2,1)}, bf16[2048,512]{1,0:T(8,128)(2,1)}, f32[8,512]{1,0:T(8,128)}) custom-call(f32[2048,512]{1,0:T(8,128)} %x_hbm.1, f32[256,640]{1,0:T(8,128)} %constant.12.clone.w_ref, bf16[256,512]{1,0:T(8,128)(2,1)} %constant.13.clone.left, bf16[512,256]{1,0:T(8,128)(2,1)} %constant.14.clone.right, f32[256,256]{1,0:T(8,128)} %constant.15.clone.inv_ref), custom_call_target="tpu_custom_call" | custom-call | tf_op jit(solution)/shard_map/chain/pallas_call | solution.py:305
  22.0 10.1 %finish.1 = f32[2048,512]{1,0:T(8,128)} custom-call(bf16[2048,512]{1,0:T(8,128)(2,1)} %get-tuple-element.8.high_hbm, bf16[2048,512]{1,0:T(8,128)(2,1)} %get-tuple-element.9.low_hbm, f32[8,512]{1,0:T(8,128)} %get-tuple-element.10.off_ref, bf16[256,512]{1,0:T(8,128)(2,1)} %constant.16.clone.left, bf16[512,256]{1,0:T(8,128)(2,1)} %constant.17.clone.right), custom_call_target="tpu_custom_call" | custom-call | tf_op jit(solution)/shard_map/finish/pallas_call | solution.py:346

commit v2 on v1

--- a/solution.py
+++ b/solution.py
@@ -15,8 +15,8 @@
 LANES = 128
 
 
-def wrap_angle(values):
-    return values - FULL_TURN * jnp.floor(values * (1.0 / FULL_TURN) + 0.5)
+def wrap_turns(values):
+    return values - jnp.round(values)
 
 
 def cos32(angle):
@@ -58,13 +58,30 @@
     return jnp.concatenate([high, low, high], axis)
 
 
+BLOCKS = TILE // LANES
+
+
+def wide(ref, first, rows):
+    return jnp.concatenate([ref[first + l, rows, :] for l in range(BLOCKS)], 1)
+
+
+def put_wide(ref, first, rows, values):
+    for l in range(values.shape[1] // LANES):
+        ref[first + l, rows, :] = values[:, l * LANES : (l + 1) * LANES]
+
+
+def in_blocks(table):
+    return np.ascontiguousarray(
+        table.reshape(table.shape[0], -1, LANES).transpose(1, 0, 2))
+
+
 def sandwich(high, low, right, left):
-    n = high.shape[0]
-    table = right[...]
-    inner = dot(stack3(high, low, 1), jnp.concatenate([table[:n], table], 0))
+    first, second = pl.ds(0, TILE), pl.ds(TILE, TILE)
+    table = [wide(right, 0, first), wide(right, 0, first), wide(right, 0, second)]
+    inner = dot(stack3(high, low, 1), jnp.concatenate(table, 0))
     high, low = split(inner)
-    table = left[...]
-    return dot(jnp.concatenate([table[:, :n], table], 1), stack3(high, low, 0))
+    table = [wide(left, 0, first), wide(left, 0, first), wide(left, BLOCKS, first)]
+    return dot(jnp.concatenate(table, 1), stack3(high, low, 0))
 
 
 def band_rows(i):
@@ -73,7 +90,8 @@
 
 def band_copy(src, dst, sem, i):
     rows = band_rows(i)
-    return pltpu.make_async_copy(src.at[rows, :], dst.at[rows, :], sem.at[i])
+    view = lambda ref: ref.at[rows, :] if len(ref.shape) == 2 else ref.at[:, rows, :]
+    return pltpu.make_async_copy(view(src), view(dst), sem.at[i])
 
 
 def finish_kernel(
@@ -91,7 +109,8 @@
         band_copy(low_hbm, low_s, low_sem, i).wait()
         for t in range(tiles):
             cols = slice(t * TILE, (t + 1) * TILE)
-            solved = sandwich(high_s[rows, cols], low_s[rows, cols], right, left)
+            high, low = wide(high_s, t * BLOCKS, rows), wide(low_s, t * BLOCKS, rows)
+            solved = sandwich(high, low, right, left)
             out_s[rows, cols] = solved + off_ref[pl.ds(i, 1), cols]
         band_copy(out_s, out_hbm, out_sem, i).start()
         return carry
@@ -130,14 +149,14 @@
     before = jnp.zeros((1, width), jnp.float32)
     for k in range(TILE // CHUNK):
         rows = pl.ds(base + k * CHUNK, CHUNK)
-        x = x_s[rows, :]
+        x = x_s[rows, :] * (1.0 / FULL_TURN)
         below = pltpu.roll(x, CHUNK - 1, 0)
         if k < TILE // CHUNK - 1:
-            below = jnp.where(row_id == CHUNK - 1, x_s[pl.ds(base + (k + 1) * CHUNK, 1), :], below)
-        down = wrap_angle(below - x)
+            below = jnp.where(row_id == CHUNK - 1, x_s[pl.ds(base + (k + 1) * CHUNK, 1), :] * (1.0 / FULL_TURN), below)
+        down = wrap_turns(below - x)
         if k == TILE // CHUNK - 1:
             down = jnp.where(row_id == CHUNK - 1, 0.0, down)
-        across = wrap_angle(pltpu.roll(x, width - 1, 1) - x)
+        across = wrap_turns(pltpu.roll(x, width - 1, 1) - x)
         acc = acc + fold(across)
         weight = w_ref[k * CHUNK : (k + 1) * CHUNK, 2 * TILE : 2 * TILE + 2]
         acc_last = acc_last + fold(down[:, :TILE] * weight[:, 0:1])
@@ -146,8 +165,8 @@
         above = jnp.where(row_id == 0, before, pltpu.roll(down, 1, 0))
         before = down[CHUNK - 1 : CHUNK, :]
         high, low = split(down - above + across - pltpu.roll(across, 1, 1))
-        dh_s[rows, :] = high
-        dl_s[rows, :] = low
+        put_wide(dh_s, 0, rows, high)
+        put_wide(dl_s, 0, rows, low)
     sum_s[pl.ds(i, 1), :] = jnp.sum(acc, axis=0, keepdims=True)
     sum_d[pl.ds(i, 1), :] = jnp.sum(acc_last, axis=0, keepdims=True)
     sum_d[pl.ds(bands + i, 1), :] = jnp.sum(acc_first, axis=0, keepdims=True)
@@ -205,20 +224,21 @@
     def spectrum_step(i, carry):
         rows = band_rows(i)
         for t in range(tiles):
-            cols = slice(t * TILE, (t + 1) * TILE)
-            scaled = sandwich(dh_s[rows, cols], dl_s[rows, cols], right, left) * inv_ref[...]
-            sh_s[rows, cols], sl_s[rows, cols] = split(scaled)
+            high, low = wide(dh_s, t * BLOCKS, rows), wide(dl_s, t * BLOCKS, rows)
+            high, low = split(sandwich(high, low, right, left) * inv_ref[...])
+            put_wide(sh_s, t * BLOCKS, rows, high)
+            put_wide(sl_s, t * BLOCKS, rows, low)
         band_copy(sh_s, high_hbm, high_sem, i).start()
         band_copy(sl_s, low_hbm, low_sem, i).start()
         return carry
 
-    scale = 1.0 / TILE
+    scale = FULL_TURN / TILE
     down_last = lane_sum(sum_d[0:bands, :])
     down_first = lane_sum(sum_d[bands : 2 * bands, :])
     edge_top.wait()
     edge_col.wait()
     below = jnp.concatenate([first_s[1:bands, :], top_in[0:1, :]], 0)
-    border = lane_sum(wrap_angle(below - last_s[0:bands, :])) * scale
+    border = lane_sum(wrap_turns((below - last_s[0:bands, :]) * (1.0 / FULL_TURN))) * scale
     band_id = lax.broadcasted_iota(jnp.int32, (bands, 1), 0)
     next_first = jnp.concatenate([down_first[1:bands], down_first[0:1]], 0)
     jump = down_last + border - next_first
@@ -244,7 +264,7 @@
     for t in range(tiles - 1):
         end = (t + 1) * TILE
         along.append(along[-1] + lasts[t] + sums[:, end - 1 : end] * scale - firsts[t + 1])
-    edge = lane_sum(wrap_angle(col_in[...] - last_s[bands : 2 * bands, :])) * scale
+    edge = lane_sum(wrap_turns((col_in[...] - last_s[bands : 2 * bands, :]) * (1.0 / FULL_TURN))) * scale
     row_total = along[-1] + lasts[-1] + edge - firsts[0]
 
     lax.fori_loop(0, bands // 2, spectrum_step, 0)
@@ -287,13 +307,16 @@
 def per_device(n_row, n_col, x):
     height, width = x.shape
     bands = height // TILE
+    blocks = (width // LANES, height, LANES)
     cosine, inverse, weights = tables(TILE)
     high = cosine.astype(jnp.bfloat16)
     low = (cosine - high.astype(np.float32)).astype(jnp.bfloat16)
-    beside, over = np.concatenate([high, low], 1), np.concatenate([high, low], 0)
-    beside_t = np.concatenate([high.T, low.T], 1)
-    over_t = np.concatenate([high.T, low.T], 0)
+    beside = in_blocks(np.concatenate([high, low], 1))
+    over = in_blocks(np.concatenate([high, low], 0))
+    beside_t = in_blocks(np.concatenate([high.T, low.T], 1))
+    over_t = in_blocks(np.concatenate([high.T, low.T], 0))
     w = np.zeros((TILE, 2 * TILE + LANES), np.float32)
+    weights = weights * np.float32(FULL_TURN)
     w[:, 0:TILE] = weights[0]
     w[:, TILE : 2 * TILE] = weights[1]
     w[:, 2 * TILE] = weights[0]
@@ -305,18 +328,18 @@
     high_s, low_s, offsets = pl.pallas_call(
         functools.partial(chain_kernel, n_row, n_col),
         out_shape=[
-            jax.ShapeDtypeStruct(x.shape, bf16),
-            jax.ShapeDtypeStruct(x.shape, bf16),
+            jax.ShapeDtypeStruct(blocks, bf16),
+            jax.ShapeDtypeStruct(blocks, bf16),
             jax.ShapeDtypeStruct((bands, width), f32),
         ],
         in_specs=[anywhere] + [vmem] * 4,
         out_specs=[anywhere, anywhere, vmem],
         scratch_shapes=[
             pltpu.VMEM((height, width), f32),
-            pltpu.VMEM((height, width), bf16),
-            pltpu.VMEM((height, width), bf16),
-            pltpu.VMEM((height, width), bf16),
-            pltpu.VMEM((height, width), bf16),
+            pltpu.VMEM(blocks, bf16),
+            pltpu.VMEM(blocks, bf16),
+            pltpu.VMEM(blocks, bf16),
+            pltpu.VMEM(blocks, bf16),
             pltpu.VMEM((bands, TILE), f32),
             pltpu.VMEM((bands, TILE), f32),
             pltpu.VMEM((8, TILE), f32),
@@ -341,7 +364,7 @@
         ],
         compiler_params=pltpu.CompilerParams(collective_id=0, has_side_effects=True),
         name="chain",
-    )(x, jnp.asarray(w), jnp.asarray(beside), jnp.asarray(over_t), jnp.asarray(inverse))
+    )(x, jnp.asarray(w), jnp.asarray(beside), jnp.asarray(over_t), jnp.asarray(inverse * np.float32(FULL_TURN)))
 
     return pl.pallas_call(
         finish_kernel,
@@ -349,8 +372,8 @@
         in_specs=[anywhere, anywhere, vmem, vmem, vmem],
         out_specs=anywhere,
         scratch_shapes=[
-            pltpu.VMEM((height, width), bf16),
-            pltpu.VMEM((height, width), bf16),
+            pltpu.VMEM(blocks, bf16),
+            pltpu.VMEM(blocks, bf16),
             pltpu.VMEM((height, width), f32),
             pltpu.SemaphoreType.DMA((bands,)),
             pltpu.SemaphoreType.DMA((bands,)),

time: 32.3 us -> 32.1 us (level)
  no operation moved by 1% of the time
where the time goes in v2:
time: 32.1 us; the launch traced here: 31.9 us
  Pallas kernels  31.9 us (99%)
    pallas_call x1, Pallas kernels, per_device(): pl.pallas_call(functools.partial(chain_kernel, n_row, n_col), out_shape=[...  21.8 us
    pallas_call x1, Pallas kernels, per_device(): pl.pallas_call(finish_kernel, out_shape=jax.ShapeDtypeStruct(x.shape, f32...  10.1 us

profile of v2, /device:TPU:0, one launch (start us, length us, event | category | flops | bytes accessed | tf_op | source)
XLA Modules:
  0.0 31.9 jit_solution(797279848033231770)
XLA Ops:
  0.0 21.8 %chain.1 = (bf16[4,2048,128]{2,1,0:T(8,128)(2,1)}, bf16[4,2048,128]{2,1,0:T(8,128)(2,1)}, f32[8,512]{1,0:T(8,128)}) custom-call(f32[2048,512]{1,0:T(8,128)} %x_hbm.1, f32[256,640]{1,0:T(8,128)} %constant.12.clone.w_ref, bf16[4,256,128]{2,1,0:T(8,128)(2,1)} %constant.13.clone.left, bf16[2,512,128]{2,1,0:T(8,128)(2,1)} %constant.14.clone.right, ...), custom_call_target="tpu_custom_call" | custom-call | tf_op jit(solution)/shard_map/chain/pallas_call | solution.py:328
  21.8 10.1 %finish.1 = f32[2048,512]{1,0:T(8,128)} custom-call(bf16[4,2048,128]{2,1,0:T(8,128)(2,1)} %get-tuple-element.8.high_hbm, bf16[4,2048,128]{2,1,0:T(8,128)(2,1)} %get-tuple-element.9.low_hbm, f32[8,512]{1,0:T(8,128)} %get-tuple-element.10.off_ref, bf16[4,256,128]{2,1,0:T(8,128)(2,1)} %constant.16.clone.left, bf16[2,512,128]{2,1,0:T(8,128)(2,1)} %constant.17.clone.right), custom_call_target="tpu_custom_call" | custom-call | tf_op jit(solution)/shard_map/finish/pallas_call | solution.py:369

commit v3 on v2

--- a/solution.py
+++ b/solution.py
@@ -75,13 +75,18 @@
         table.reshape(table.shape[0], -1, LANES).transpose(1, 0, 2))
 
 
-def sandwich(high, low, right, left):
+def sandwich(pairs, right, left):
     first, second = pl.ds(0, TILE), pl.ds(TILE, TILE)
     table = [wide(right, 0, first), wide(right, 0, first), wide(right, 0, second)]
-    inner = dot(stack3(high, low, 1), jnp.concatenate(table, 0))
-    high, low = split(inner)
+    table = jnp.concatenate(table, 0)
+    inner = [split(dot(stack3(high, low, 1), table)) for high, low in pairs]
     table = [wide(left, 0, first), wide(left, 0, first), wide(left, BLOCKS, first)]
-    return dot(jnp.concatenate(table, 1), stack3(high, low, 0))
+    table = jnp.concatenate(table, 1)
+    return [dot(table, stack3(high, low, 0)) for high, low in inner]
+
+
+def group_size(bands, most):
+    return next(g for g in range(most, 0, -1) if bands % g == 0)
 
 
 def band_rows(i):
@@ -103,19 +108,26 @@
         band_copy(high_hbm, high_s, high_sem, i).start()
         band_copy(low_hbm, low_s, low_sem, i).start()
 
-    def step(i, carry):
-        rows = band_rows(i)
-        band_copy(high_hbm, high_s, high_sem, i).wait()
-        band_copy(low_hbm, low_s, low_sem, i).wait()
-        for t in range(tiles):
+    group = group_size(bands, 2)
+
+    def step(j, carry):
+        some = [j * group + k for k in range(group)]
+        for i in some:
+            band_copy(high_hbm, high_s, high_sem, i).wait()
+            band_copy(low_hbm, low_s, low_sem, i).wait()
+        places = [(i, t) for i in some for t in range(tiles)]
+        pairs = [
+            (wide(high_s, t * BLOCKS, band_rows(i)), wide(low_s, t * BLOCKS, band_rows(i)))
+            for i, t in places
+        ]
+        for (i, t), solved in zip(places, sandwich(pairs, right, left)):
             cols = slice(t * TILE, (t + 1) * TILE)
-            high, low = wide(high_s, t * BLOCKS, rows), wide(low_s, t * BLOCKS, rows)
-            solved = sandwich(high, low, right, left)
-            out_s[rows, cols] = solved + off_ref[pl.ds(i, 1), cols]
-        band_copy(out_s, out_hbm, out_sem, i).start()
+            out_s[band_rows(i), cols] = solved + off_ref[pl.ds(i, 1), cols]
+        for i in some:
+            band_copy(out_s, out_hbm, out_sem, i).start()
         return carry
 
-    lax.fori_loop(0, bands, step, 0)
+    lax.fori_loop(0, bands // group, step, 0)
     for i in range(bands):
         band_copy(out_s, out_hbm, out_sem, i).wait()
 
@@ -221,15 +233,22 @@
 
     lax.fori_loop(0, bands, slope_step, 0)
 
-    def spectrum_step(i, carry):
-        rows = band_rows(i)
-        for t in range(tiles):
-            high, low = wide(dh_s, t * BLOCKS, rows), wide(dl_s, t * BLOCKS, rows)
-            high, low = split(sandwich(high, low, right, left) * inv_ref[...])
-            put_wide(sh_s, t * BLOCKS, rows, high)
-            put_wide(sl_s, t * BLOCKS, rows, low)
-        band_copy(sh_s, high_hbm, high_sem, i).start()
-        band_copy(sl_s, low_hbm, low_sem, i).start()
+    group = group_size(bands // 2, 4)
+
+    def spectrum_step(j, carry):
+        some = [j * group + k for k in range(group)]
+        places = [(i, t) for i in some for t in range(tiles)]
+        pairs = [
+            (wide(dh_s, t * BLOCKS, band_rows(i)), wide(dl_s, t * BLOCKS, band_rows(i)))
+            for i, t in places
+        ]
+        for (i, t), spectrum in zip(places, sandwich(pairs, right, left)):
+            high, low = split(spectrum * inv_ref[...])
+            put_wide(sh_s, t * BLOCKS, band_rows(i), high)
+            put_wide(sl_s, t * BLOCKS, band_rows(i), low)
+        for i in some:
+            band_copy(sh_s, high_hbm, high_sem, i).start()
+            band_copy(sl_s, low_hbm, low_sem, i).start()
         return carry
 
     scale = FULL_TURN / TILE
@@ -267,7 +286,8 @@
     edge = lane_sum(wrap_turns((col_in[...] - last_s[bands : 2 * bands, :]) * (1.0 / FULL_TURN))) * scale
     row_total = along[-1] + lasts[-1] + edge - firsts[0]
 
-    lax.fori_loop(0, bands // 2, spectrum_step, 0)
+    half = bands // 2 // group
+    lax.fori_loop(0, half, spectrum_step, 0)
     for copy in copies:
         copy.wait()
     above = jnp.zeros((1, 1), jnp.float32)
@@ -289,7 +309,7 @@
             device_id=(r, lax.rem(c + k, n_col)), device_id_type=MESH))
     for copy in copies:
         copy.start()
-    lax.fori_loop(bands // 2, bands, spectrum_step, 0)
+    lax.fori_loop(half, bands // group, spectrum_step, 0)
     for copy in copies:
         copy.wait()
     offset = jnp.where(c == 0, starts + firsts[0], 0.0) - firsts[0]

time: 32.1 us -> 29 us (0.903)
  Pallas kernels: 31.9 us -> 28.8 us
    pallas_call x1, Pallas kernels: 10.1 us -> 7.36 us  [per_device(): pl.pallas_call(finish_kernel, out_shape=jax.ShapeDtypeStruct(x.shape, f32...]
    pallas_call x1, Pallas kernels: 21.8 us -> 21.5 us  [per_device(): pl.pallas_call(functools.partial(chain_kernel, n_row, n_col), out_shape=[...]
where the time goes in v3:
time: 29 us; the launch traced here: 28.8 us
  Pallas kernels  28.8 us (99%)
    pallas_call x1, Pallas kernels, per_device(): pl.pallas_call(functools.partial(chain_kernel, n_row, n_col), out_shape=[...  21.5 us
    pallas_call x1, Pallas kernels, per_device(): pl.pallas_call(finish_kernel, out_shape=jax.ShapeDtypeStruct(x.shape, f32...  7.36 us

profile of v3, /device:TPU:0, one launch (start us, length us, event | category | flops | bytes accessed | tf_op | source)
XLA Modules:
  0.0 28.8 jit_solution(12583288037592426306)
XLA Ops:
  0.0 21.5 %chain.1 = (bf16[4,2048,128]{2,1,0:T(8,128)(2,1)}, bf16[4,2048,128]{2,1,0:T(8,128)(2,1)}, f32[8,512]{1,0:T(8,128)}) custom-call(f32[2048,512]{1,0:T(8,128)} %x_hbm.1, f32[256,640]{1,0:T(8,128)} %constant.12.clone.w_ref, bf16[4,256,128]{2,1,0:T(8,128)(2,1)} %constant.13.clone.left, bf16[2,512,128]{2,1,0:T(8,128)(2,1)} %constant.14.clone.right, ...), custom_call_target="tpu_custom_call" | custom-call | tf_op jit(solution)/shard_map/chain/pallas_call | solution.py:348
  21.5 7.4 %finish.1 = f32[2048,512]{1,0:T(8,128)} custom-call(bf16[4,2048,128]{2,1,0:T(8,128)(2,1)} %get-tuple-element.8.high_hbm, bf16[4,2048,128]{2,1,0:T(8,128)(2,1)} %get-tuple-element.9.low_hbm, f32[8,512]{1,0:T(8,128)} %get-tuple-element.10.off_ref, bf16[4,256,128]{2,1,0:T(8,128)(2,1)} %constant.16.clone.left, bf16[2,512,128]{2,1,0:T(8,128)(2,1)} %constant.17.clone.right), custom_call_target="tpu_custom_call" | custom-call | tf_op jit(solution)/shard_map/finish/pallas_call | solution.py:389
